TPU v7x, 32 devices: a whole 2x2x4 slice. The times are simulated.
32 devices in a mesh: row: 4 (over y, core), col: 8 (over z, x).
Axes of the slice: x: 2, y: 2, z: 4, core: 2. Of those that a mesh axis runs over, the one named last changes fastest.
Arguments:
- amplitudes: float32 [2, 32, 1048576], P(None, 'row', 'col'), may hold values from -6 to 6
- qubit_order: int32 [11], replicated, may hold values from 0 to 10, each once
Outputs:
- correlators: float32 [8, 131072], P('col', 'row')
Inputs may be any that keep to these rules, and one draw needn't show every extreme that they name: `qubit_order`: a permutation of 0 to 10.
All inputs are finite; a program needn't handle non-finite values.
Results may differ from a plain program's by a relative error of at most 0.0003.
Values sent between devices are 32-bit elements; how exact they have to be, the bound alone decides.
No kernel may reach another device: no remote copies, remote signals or barrier semaphores. Data moves between devices by JAX's collectives and lax.ppermute only.
A program may use at most 64 MiB of HBM per device.

v0:
```python
import functools

import jax
import jax.numpy as jnp
from jax import lax
from jax.experimental import pallas as pl
from jax.experimental.pallas import tpu as pltpu
from jax.sharding import PartitionSpec as P


LANES = 128
FIRST_PART = 5
SUB = 8
ROW_SIDE = 16
CHUNK = ROW_SIDE * ROW_SIDE * LANES


def log2(n):
    return n.bit_length() - 1


def parity_sign(common, bits):
    shift = 1
    while shift < bits:
        common = jnp.bitwise_xor(common, jnp.right_shift(common, shift))
        shift *= 2
    return (1 - 2 * jnp.bitwise_and(common, 1)).astype(jnp.float32)


def first_rows(share):
    unit = 4 * SUB if share % (8 * SUB) == 0 else SUB
    return share * FIRST_PART // 8 // unit * unit


def block_order(count):
    order = [0]
    for k in reversed(range(log2(count))):
        order = order + [j + (1 << k) for j in order]
    return order


def iota(shape, axis):
    return lax.broadcasted_iota(jnp.int32, shape, axis)


def bit_of(values, position):
    return jnp.bitwise_and(jnp.right_shift(values, position), 1)


def split(values):
    high = values.astype(jnp.bfloat16)
    low = (values - high.astype(jnp.float32)).astype(jnp.bfloat16)
    return jnp.concatenate([high, low], axis=1)


def transform_kernel(
    row_axis, order_in, amps, messages, buf, out, xs, hlane,
    order, inverse, rows_moved, lanes_moved, row_target, row_unit, lane_unit, order_sem, sems,
):
    parts, groups, length = buf.shape[0], buf.shape[1] // SUB, buf.shape[2]
    chunks = length // CHUNK
    half = CHUNK // 2
    side = ROW_SIDE * ROW_SIDE
    lane_bits, row_bits = log2(LANES), log2(ROW_SIDE)
    count = order.shape[0]

    def copies(step):
        return [
            pltpu.make_async_copy(
                amps.at[p, :, pl.ds(step * half, half)], buf.at[p, :, pl.ds(step * half, half)], sems.at[step, p]
            )
            for p in range(parts)
        ]

    order_copy = pltpu.make_async_copy(order_in, order, order_sem)
    order_copy.start()
    for step in range(2 * chunks):
        for copy in copies(step):
            copy.start()

    stacked = (2 * LANES, LANES)
    lane_sign = parity_sign(
        jnp.bitwise_and(jnp.bitwise_and(iota(stacked, 0), LANES - 1), iota(stacked, 1)), lane_bits
    )
    hlane[...] = lane_sign.astype(jnp.bfloat16)
    for p in range(count + 1):
        rows_moved[p] = lane_bits
        lanes_moved[p] = 0
    for r in range(row_bits + 1):
        lane_unit[r] = 0
    order_copy.wait()

    for j in range(count):
        inverse[order[j]] = j
    rank = jnp.int32(0)
    for p in range(lane_bits):
        lanes_moved[rank] = p
        rank = rank + (inverse[p] >= lane_bits).astype(jnp.int32)
    lane = iota((1, LANES), 1)
    lane_index = row_flip = out_row_flip = jnp.zeros((1, LANES), jnp.int32)
    rank = jnp.int32(0)
    for p in range(lane_bits, count):
        goes_to = inverse[p]
        crosses = goes_to < lane_bits
        rows_moved[rank] = p
        target = inverse[jnp.where(crosses, lanes_moved[rank], p)] - lane_bits
        row_target[p - lane_bits] = target
        row_unit[target] = 1 << p - lane_bits
        flip = jnp.left_shift(bit_of(lane, jnp.where(crosses, goes_to, 0)), target)
        out_row_flip = out_row_flip + jnp.where(crosses, flip, 0)
        rank = rank + crosses.astype(jnp.int32)
    rank = jnp.int32(0)
    for p in range(lane_bits):
        crosses = inverse[p] >= lane_bits
        partner = rows_moved[rank]
        lane_index = lane_index + jnp.left_shift(bit_of(lane, inverse[jnp.where(crosses, partner, p)]), p)
        target = row_target[jnp.where(crosses, partner - lane_bits, 0)]
        row_flip = row_flip + jnp.where(crosses, jnp.left_shift(bit_of(lane, p), target), 0)
        lane_unit[jnp.where(crosses, target, row_bits)] = 1 << p
        rank = rank + crosses.astype(jnp.int32)

    flips = [bit_of(row_flip, r) == 1 for r in range(row_bits)]
    out_flips = [bit_of(out_row_flip, r) == 1 for r in range(row_bits)]
    sources, gathers = [jnp.int32(0)], [jnp.int32(0)]
    for r in range(row_bits):
        sources = sources + [source + row_unit[r] for source in sources]
        gathers = gathers + [gather + lane_unit[r] for gather in gathers]
    gathers = [jnp.broadcast_to(jnp.bitwise_xor(lane_index, gather), (ROW_SIDE, LANES)) for gather in gathers]

    sub = iota((SUB, LANES), 0)
    masks = [bit_of(sub, level) == 0 for level in range(log2(SUB))]

    def packed_row(base, i):
        tiles = []
        for s in range(SUB):
            start = base + (s * ROW_SIDE + i) * LANES
            total = None
            for p in range(parts):
                for g in range(groups):
                    v = buf[p, g * SUB : (g + 1) * SUB, pl.ds(start, LANES)]
                    total = v * v if total is None else total + v * v
            tiles.append(total)
        for level in range(log2(SUB)):
            merged = []
            for k in range(0, len(tiles), 2):
                a, b = tiles[k] + tiles[k + 1], tiles[k] - tiles[k + 1]
                here = jnp.where(masks[level], a, b)
                other = jnp.where(masks[level], b, a)
                merged.append(here + pltpu.roll(other, SUB - (1 << level), 0))
            tiles = merged
        return tiles[0]

    def flip_rows(rows, which):
        for r in range(row_bits):
            rows = [jnp.where(which[r], rows[i ^ 1 << r], rows[i]) for i in range(ROW_SIDE)]
        return rows

    def butterfly(blocks, stride):
        return [
            blocks[c ^ stride] - blocks[c] if c & stride else blocks[c] + blocks[c ^ stride] for c in range(len(blocks))
        ]

    def arrive(step):
        for copy in copies(step):
            copy.wait()

    def sums(step, upper, total):
        base = pl.multiple_of(step * half, half)
        for i in range(ROW_SIDE):
            packed = packed_row(base, i)
            total = total + packed
            xs[i, upper * SUB : (upper + 1) * SUB, :] = packed
        return total

    def transform(c):
        rows = flip_rows([xs[source] for source in sources], flips)
        rows = [jnp.take_along_axis(rows[i], gathers[i], axis=1) for i in range(ROW_SIDE)]
        rows = flip_rows(rows, out_flips)
        for r in range(row_bits):
            rows = butterfly(rows, 1 << r)
        rows = [
            jnp.concatenate(butterfly([row[upper * SUB : (upper + 1) * SUB] for upper in range(2)], 1), axis=0)
            for row in rows
        ]
        z = jnp.dot(split(jnp.concatenate(rows, axis=0)), hlane[...], preferred_element_type=jnp.float32)
        first = pl.multiple_of(c * side, side)
        for i in range(ROW_SIDE):
            out[pl.ds(first + i, ROW_SIDE, stride=ROW_SIDE), :] = z[i * ROW_SIDE : (i + 1) * ROW_SIDE]

    def one_chunk(c, total):
        arrive(2 * c)
        transform(c - 1)
        total = sums(2 * c, 0, total)
        arrive(2 * c + 1)
        return sums(2 * c + 1, 1, total)

    total = jnp.zeros((SUB, LANES), jnp.float32)
    for upper in range(2):
        arrive(upper)
        total = sums(upper, upper, total)
    total = lax.fori_loop(1, chunks, one_chunk, total)
    transform(chunks - 1)
    total = jnp.broadcast_to(jnp.sum(total[:1], keepdims=True), (SUB, LANES))

    blocks = lax.axis_size(row_axis)
    share = out.shape[0] // blocks
    own = lax.axis_index(row_axis)
    order_of_blocks = block_order(blocks)
    first = first_rows(share)

    def place(j, row):
        at = order_of_blocks.index(j)
        if row < first:
            return at * (first + SUB) + row
        return blocks * (first + SUB) + at * (share - first) + row - first

    signs = [parity_sign(jnp.bitwise_and(own, c), log2(blocks)) for c in range(chunks)]
    rows = 4 * SUB
    for start in range(0, side, rows):
        levels = [out[c * side + start : c * side + start + rows, :] for c in range(chunks)]
        if blocks == chunks:
            levels = [levels[0]] + [signs[c] * levels[c] for c in range(1, chunks)]
        for k in range(log2(chunks)):
            levels = butterfly(levels, 1 << k)
        for c in range(chunks):
            if blocks == chunks:
                messages[place(c, start) : place(c, start) + rows, :] = levels[c]
            else:
                out[c * side + start : c * side + start + rows, :] = levels[c]
    if blocks != chunks:
        for j in range(blocks):
            source = jnp.bitwise_xor(own, j) * share
            for low, size in ((0, first), (first, share - first)):
                rows_in = pl.ds(pl.multiple_of(source + low, SUB), size)
                messages[place(j, low) : place(j, low) + size, :] = out[rows_in, :]
    for k in range(blocks):
        at = k * (first + SUB) + first
        messages[at : at + SUB, :] = total


def transform_local(amplitudes, qubit_order, row_axis):
    parts, unmeasured, length = amplitudes.shape
    chunks = length // CHUNK
    side = ROW_SIDE * ROW_SIDE
    count = qubit_order.shape[0]
    return pl.pallas_call(
        functools.partial(transform_kernel, row_axis),
        out_shape=pltpu.VMEM((chunks * side + lax.axis_size(row_axis) * SUB, LANES), jnp.float32),
        in_specs=[pl.BlockSpec(memory_space=pl.ANY), pl.BlockSpec(memory_space=pl.ANY)],
        out_specs=pl.BlockSpec(memory_space=pltpu.VMEM),
        scratch_shapes=[
            pltpu.VMEM((parts, unmeasured, length), jnp.float32),
            pltpu.VMEM((chunks * side, LANES), jnp.float32),
            pltpu.VMEM((ROW_SIDE, ROW_SIDE, LANES), jnp.float32),
            pltpu.VMEM((2 * LANES, LANES), jnp.bfloat16),
            pltpu.SMEM((count,), jnp.int32),
            *[pltpu.SMEM((count + 1,), jnp.int32) for _ in range(6)],
            pltpu.SemaphoreType.DMA(()),
            pltpu.SemaphoreType.DMA((2 * chunks, parts)),
        ],
        name="transform_local",
    )(qubit_order, amplitudes)


def exchange(message, row_mask, col_mask):
    rows, cols = lax.axis_size("row"), lax.axis_size("col")
    mask = row_mask * cols + col_mask
    return lax.ppermute(message, ("row", "col"), [(i, i ^ mask) for i in range(rows * cols)])


def pick_of(bits, pick):
    return sum(1 << b for k, b in enumerate(bits) if pick >> k & 1)


def run_steps(blocks, steps, tail):
    for row_bits, col_bits in steps:
        dropped = pick_of(row_bits, -1)
        left = [j for j in blocks if j & dropped == 0]
        size = blocks[0].shape[0]
        signs = [1.0 - 2.0 * bit_of(lax.axis_index("col"), b).astype(jnp.float32) for b in col_bits]
        terms = []
        for row_pick in range(1 << len(row_bits)):
            row_mask = pick_of(row_bits, row_pick)
            joined = [blocks[j ^ row_mask] for j in left]
            message = joined[0] if len(joined) == 1 else jnp.concatenate(joined)
            for pick in range(1 << len(col_bits)):
                col_mask = pick_of(col_bits, pick)
                term = message
                if row_mask or col_mask:
                    term = exchange(message, row_mask, col_mask)
                terms.append((pick, term))
        blocks = {}
        for k, j in enumerate(left):
            values, summed = None, None
            for pick, term in terms:
                term = term[k * size : (k + 1) * size]
                part = term[: size - tail] if col_bits else term
                for n in range(len(col_bits)):
                    if not pick >> n & 1:
                        part = part * signs[n]
                values = part if values is None else values + part
                if tail and col_bits:
                    summed = term[size - tail :] if summed is None else summed + term[size - tail :]
            blocks[j] = jnp.concatenate([values, summed]) if tail and col_bits else values
    return blocks[0]


def local(amplitudes, qubit_order, measured_qubits):
    messages = transform_local(amplitudes, qubit_order, "row")
    count = lax.axis_size("row")
    row_bits, col_bits = log2(count), log2(lax.axis_size("col"))
    share = messages.shape[0] // count - SUB
    first = first_rows(share)
    first_blocks, second_blocks = {}, {}
    order_of_blocks = block_order(count)
    for at, j in enumerate(order_of_blocks):
        first_blocks[j] = messages[at * (first + SUB) : (at + 1) * (first + SUB)]
        start = count * (first + SUB) + at * (share - first)
        second_blocks[j] = messages[start : start + share - first]

    later = [((k,), ()) for k in range(2, row_bits)]
    first_steps = [((0,), ()), ((1,), (0,))] + later + [((), (b,)) for b in range(1, col_bits)]
    others = list(range(col_bits - 1))
    second_steps = [((0, 1), ())] + later + [((), (col_bits - 1,))]
    second_steps += [((), tuple(others[k : k + 2])) for k in range(0, len(others), 2)]
    one = run_steps(first_blocks, first_steps, SUB)
    two = run_steps(second_blocks, second_steps, 0)
    total = one[-SUB : 1 - SUB]
    values = jnp.concatenate([one[:-SUB], two])
    return (values * 2.0 ** (measured_qubits / 2) / total).reshape(1, -1)


def solution(mesh):
    def program(amplitudes, qubit_order):
        measured_qubits = log2(amplitudes.shape[2])

        def body(a, q):
            return local(a, q, measured_qubits)

        return jax.shard_map(
            body,
            mesh=mesh,
            in_specs=(P(None, "row", "col"), P()),
            out_specs=P("col", "row"),
            check_vma=False,
        )(amplitudes, qubit_order)

    return program
```

profile of v0, /device:TPU:0, one launch (start us, length us, event | category | flops | bytes accessed | tf_op | source)
XLA Modules:
  0.0 27.2 jit_solution(17160759783596571372)
XLA Ops:
  0.0 4.3 %transform_local.1 = f32[1056,128]{1,0:T(8,128)S(1)} custom-call(s32[11]{0:T(128)} %order_in.1, f32[2,8,131072]{2,1,0:T(8,128)} %amps.1), custom_call_target="tpu_custom_call" | custom-call | tf_op jit(solution)/shard_map/transform_local/pallas_call | solution.py:246
  4.3 0.6 %collective-permute-start = (f32[336,128]{1,0:T(8,128)S(1)}, f32[336,128]{1,0:T(8,128)S(1)}, u32[]{:S(2)}, u32[]{:S(2)}) collective-permute-start(f32[336,128]{1,0:T(8,128)S(1)} %concatenate.16), channel_id=1, source_target_pairs={{0,8},{1,9},{2,10},{3,11},{4,12},{5,13},{6,14},{7,15},{8,0},{9,1},... | collective-permute-start | bytes 516104 | tf_op jit(solution)/shard_map/ppermute | solution.py:268
  4.9 0.1 collective-permute-start.6
  5.0 2.7 %collective-permute-start.8 = (f32[96,128]{1,0:T(8,128)S(1)}, f32[96,128]{1,0:T(8,128)S(1)}, u32[]{:S(2)}, u32[]{:S(2)}) collective-permute-start(f32[96,128]{1,0:T(8,128)S(1)} %get-tuple-element.8), channel_id=1, source_target_pairs={{0,24},{1,25},{2,26},{3,27},{4,28},{5,29},{6,30},{7,31},{8,16},{9,... | collective-permute-start | bytes 147464 | tf_op jit(solution)/shard_map/ppermute | solution.py:268
  7.7 0.3 %collective-permute-start.7 = (f32[96,128]{1,0:T(8,128)S(1)}, f32[96,128]{1,0:T(8,128)S(1)}, u32[]{:S(2)}, u32[]{:S(2)}) collective-permute-start(f32[96,128]{1,0:T(8,128)S(1)} %get-tuple-element.9), channel_id=1, source_target_pairs={{0,16},{1,17},{2,18},{3,19},{4,20},{5,21},{6,22},{7,23},{8,24},{9,... | collective-permute-start | bytes 147464 | tf_op jit(solution)/shard_map/ppermute | solution.py:268
  8.0 0.0 collective-permute-done
  8.0 2.7 %collective-permute-start.3 = (f32[168,128]{1,0:T(8,128)S(1)}, f32[168,128]{1,0:T(8,128)S(1)}, u32[]{:S(2)}, u32[]{:S(2)}) collective-permute-start(f32[168,128]{1,0:T(8,128)S(1)} %get-tuple-element.6), channel_id=1, source_target_pairs={{0,17},{1,16},{2,19},{3,18},{4,21},{5,20},{6,23},{7,22},{8,25},{9,... | collective-permute-start | bytes 258056 | tf_op jit(solution)/shard_map/ppermute | solution.py:268
  10.7 0.5 %collective-permute-start.2 = (f32[168,128]{1,0:T(8,128)S(1)}, f32[168,128]{1,0:T(8,128)S(1)}, u32[]{:S(2)}, u32[]{:S(2)}) collective-permute-start(f32[168,128]{1,0:T(8,128)S(1)} %get-tuple-element.6), channel_id=1, source_target_pairs={{0,16},{1,17},{2,18},{3,19},{4,20},{5,21},{6,22},{7,23},{8,24},{9,... | collective-permute-start | bytes 258056 | tf_op jit(solution)/shard_map/ppermute | solution.py:268
  11.2 0.0 collective-permute-done.6
  11.2 0.3 %collective-permute-start.1 = (f32[168,128]{1,0:T(8,128)S(1)}, f32[168,128]{1,0:T(8,128)S(1)}, u32[]{:S(2)}, u32[]{:S(2)}) collective-permute-start(f32[168,128]{1,0:T(8,128)S(1)} %get-tuple-element.5), channel_id=1, source_target_pairs={{0,1},{1,0},{2,3},{3,2},{4,5},{5,4},{6,7},{7,6},{8,9},{9,8},{10,11... | collective-permute-start | bytes 258056 | tf_op jit(solution)/shard_map/ppermute | solution.py:268
  11.6 0.0 collective-permute-done.8
  11.6 0.2 collective-permute-done.7
  11.8 2.7 %collective-permute-start.9 = (f32[96,128]{1,0:T(8,128)S(1)}, f32[96,128]{1,0:T(8,128)S(1)}, u32[]{:S(2)}, u32[]{:S(2)}) collective-permute-start(f32[96,128]{1,0:T(8,128)S(1)} %fusion.3), channel_id=1, source_target_pairs={{0,4},{1,5},{2,6},{3,7},{4,0},{5,1},{6,2},{7,3},{8,12},{9,13},{10,... | collective-permute-start | bytes 147464 | tf_op jit(solution)/shard_map/ppermute | solution.py:268
  14.4 0.0 collective-permute-done.3
  14.5 1.0 %collective-permute-done.2 = f32[168,128]{1,0:T(8,128)S(1)} collective-permute-done((f32[168,128]{1,0:T(8,128)S(1)}, f32[168,128]{1,0:T(8,128)S(1)}, u32[]{:S(2)}, u32[]{:S(2)}) %collective-permute-start.2) | collective-permute-done | bytes 86048 | tf_op jit(solution)/shard_map/ppermute | solution.py:268
  15.5 0.3 collective-permute-done.1
  15.8 1.6 %collective-permute-start.4 = (f32[168,128]{1,0:T(8,128)S(1)}, f32[168,128]{1,0:T(8,128)S(1)}, u32[]{:S(2)}, u32[]{:S(2)}) collective-permute-start(f32[168,128]{1,0:T(8,128)S(1)} %pad_maximum_fusion), channel_id=1, source_target_pairs={{0,2},{1,3},{2,0},{3,1},{4,6},{5,7},{6,4},{7,5},{8,10},{9,11},{10,... | collective-permute-start | bytes 258056 | tf_op jit(solution)/shard_map/ppermute | solution.py:268
  17.4 0.0 collective-permute-done.9
  17.4 2.0 %collective-permute-start.12 = (f32[96,128]{1,0:T(8,128)S(1)}, f32[96,128]{1,0:T(8,128)S(1)}, u32[]{:S(2)}, u32[]{:S(2)}) collective-permute-start(f32[96,128]{1,0:T(8,128)S(1)} %multiply_add_fusion.1), channel_id=1, source_target_pairs={{0,3},{1,2},{2,1},{3,0},{4,7},{5,6},{6,5},{7,4},{8,11},{9,10},{10,... | collective-permute-start | bytes 147464 | tf_op jit(solution)/shard_map/ppermute | solution.py:268
  19.4 1.0 %collective-permute-start.11 = (f32[96,128]{1,0:T(8,128)S(1)}, f32[96,128]{1,0:T(8,128)S(1)}, u32[]{:S(2)}, u32[]{:S(2)}) collective-permute-start(f32[96,128]{1,0:T(8,128)S(1)} %multiply_add_fusion.1), channel_id=1, source_target_pairs={{0,2},{1,3},{2,0},{3,1},{4,6},{5,7},{6,4},{7,5},{8,10},{9,11},{10,... | collective-permute-start | bytes 147464 | tf_op jit(solution)/shard_map/ppermute | solution.py:268
  20.4 0.5 %collective-permute-start.10 = (f32[96,128]{1,0:T(8,128)S(1)}, f32[96,128]{1,0:T(8,128)S(1)}, u32[]{:S(2)}, u32[]{:S(2)}) collective-permute-start(f32[96,128]{1,0:T(8,128)S(1)} %multiply_add_fusion.1), channel_id=1, source_target_pairs={{0,1},{1,0},{2,3},{3,2},{4,5},{5,4},{6,7},{7,6},{8,9},{9,8},{10,11... | collective-permute-start | bytes 147464 | tf_op jit(solution)/shard_map/ppermute | solution.py:268
  21.0 0.0 collective-permute-done.4
  21.0 2.7 %collective-permute-start.5 = (f32[168,128]{1,0:T(8,128)S(1)}, f32[168,128]{1,0:T(8,128)S(1)}, u32[]{:S(2)}, u32[]{:S(2)}) collective-permute-start(f32[168,128]{1,0:T(8,128)S(1)} %pad_maximum_fusion.1), channel_id=1, source_target_pairs={{0,4},{1,5},{2,6},{3,7},{4,0},{5,1},{6,2},{7,3},{8,12},{9,13},{10,... | collective-permute-start | bytes 258056 | tf_op jit(solution)/shard_map/ppermute | solution.py:268
  23.7 0.0 collective-permute-done.12
  23.7 0.6 %collective-permute-done.11 = f32[96,128]{1,0:T(8,128)S(1)} collective-permute-done((f32[96,128]{1,0:T(8,128)S(1)}, f32[96,128]{1,0:T(8,128)S(1)}, u32[]{:S(2)}, u32[]{:S(2)}) %collective-permute-start.11) | collective-permute-done | bytes 49184 | tf_op jit(solution)/shard_map/ppermute | solution.py:268
  24.2 0.3 %collective-permute-done.10 = f32[96,128]{1,0:T(8,128)S(1)} collective-permute-done((f32[96,128]{1,0:T(8,128)S(1)}, f32[96,128]{1,0:T(8,128)S(1)}, u32[]{:S(2)}, u32[]{:S(2)}) %collective-permute-start.10) | collective-permute-done | bytes 49184 | tf_op jit(solution)/shard_map/ppermute | solution.py:268
  24.6 1.9 %collective-permute-done.5 = f32[168,128]{1,0:T(8,128)S(1)} collective-permute-done((f32[168,128]{1,0:T(8,128)S(1)}, f32[168,128]{1,0:T(8,128)S(1)}, u32[]{:S(2)}, u32[]{:S(2)}) %collective-permute-start.5) | collective-permute-done | bytes 86048 | tf_op jit(solution)/shard_map/ppermute | solution.py:268
  26.5 0.7 %fusion = f32[256,128]{1,0:T(8,128)} fusion(f32[96,128]{1,0:T(8,128)S(1)} %fusion.4, f32[160,128]{1,0:T(8,128)S(1)} %slice_add_fusion.2, f32[128]{0:T(128)S(1)} %slice_bitcast_fusion), kind=kLoop, calls=%fused_computation.1 | loop fusion | flops 98304 | bytes 262656 | tf_op jit(solution)/shard_map/div | solution.py:330
  (15 shorter events, 0.2 us)
Async XLA Ops:
  4.3 3.7 %collective-permute-start = (f32[336,128]{1,0:T(8,128)S(1)}, f32[336,128]{1,0:T(8,128)S(1)}, u32[]{:S(2)}, u32[]{:S(2)}) collective-permute-start(f32[336,128]{1,0:T(8,128)S(1)} %concatenate.16), channel_id=1, source_target_pairs={{0,8},{1,9},{2,10},{3,11},{4,12},{5,13},{6,14},{7,15},{8,0},{9,1},... | collective-permute-start | bytes 516104 | tf_op jit(solution)/shard_map/ppermute | solution.py:268
  4.9 6.3 %collective-permute-start.6 = (f32[96,128]{1,0:T(8,128)S(1)}, f32[96,128]{1,0:T(8,128)S(1)}, u32[]{:S(2)}, u32[]{:S(2)}) collective-permute-start(f32[96,128]{1,0:T(8,128)S(1)} %get-tuple-element.7), channel_id=1, source_target_pairs={{0,8},{1,9},{2,10},{3,11},{4,12},{5,13},{6,14},{7,15},{8,0},{9,1},... | collective-permute-start | bytes 147464 | tf_op jit(solution)/shard_map/ppermute | solution.py:268
  5.0 6.6 %collective-permute-start.8 = (f32[96,128]{1,0:T(8,128)S(1)}, f32[96,128]{1,0:T(8,128)S(1)}, u32[]{:S(2)}, u32[]{:S(2)}) collective-permute-start(f32[96,128]{1,0:T(8,128)S(1)} %get-tuple-element.8), channel_id=1, source_target_pairs={{0,24},{1,25},{2,26},{3,27},{4,28},{5,29},{6,30},{7,31},{8,16},{9,... | collective-permute-start | bytes 147464 | tf_op jit(solution)/shard_map/ppermute | solution.py:268
  7.7 4.1 %collective-permute-start.7 = (f32[96,128]{1,0:T(8,128)S(1)}, f32[96,128]{1,0:T(8,128)S(1)}, u32[]{:S(2)}, u32[]{:S(2)}) collective-permute-start(f32[96,128]{1,0:T(8,128)S(1)} %get-tuple-element.9), channel_id=1, source_target_pairs={{0,16},{1,17},{2,18},{3,19},{4,20},{5,21},{6,22},{7,23},{8,24},{9,... | collective-permute-start | bytes 147464 | tf_op jit(solution)/shard_map/ppermute | solution.py:268
  8.0 6.4 %collective-permute-start.3 = (f32[168,128]{1,0:T(8,128)S(1)}, f32[168,128]{1,0:T(8,128)S(1)}, u32[]{:S(2)}, u32[]{:S(2)}) collective-permute-start(f32[168,128]{1,0:T(8,128)S(1)} %get-tuple-element.6), channel_id=1, source_target_pairs={{0,17},{1,16},{2,19},{3,18},{4,21},{5,20},{6,23},{7,22},{8,25},{9,... | collective-permute-start | bytes 258056 | tf_op jit(solution)/shard_map/ppermute | solution.py:268
  10.7 4.7 %collective-permute-start.2 = (f32[168,128]{1,0:T(8,128)S(1)}, f32[168,128]{1,0:T(8,128)S(1)}, u32[]{:S(2)}, u32[]{:S(2)}) collective-permute-start(f32[168,128]{1,0:T(8,128)S(1)} %get-tuple-element.6), channel_id=1, source_target_pairs={{0,16},{1,17},{2,18},{3,19},{4,20},{5,21},{6,22},{7,23},{8,24},{9,... | collective-permute-start | bytes 258056 | tf_op jit(solution)/shard_map/ppermute | solution.py:268
  11.2 4.5 %collective-permute-start.1 = (f32[168,128]{1,0:T(8,128)S(1)}, f32[168,128]{1,0:T(8,128)S(1)}, u32[]{:S(2)}, u32[]{:S(2)}) collective-permute-start(f32[168,128]{1,0:T(8,128)S(1)} %get-tuple-element.5), channel_id=1, source_target_pairs={{0,1},{1,0},{2,3},{3,2},{4,5},{5,4},{6,7},{7,6},{8,9},{9,8},{10,11... | collective-permute-start | bytes 258056 | tf_op jit(solution)/shard_map/ppermute | solution.py:268
  11.8 5.6 %collective-permute-start.9 = (f32[96,128]{1,0:T(8,128)S(1)}, f32[96,128]{1,0:T(8,128)S(1)}, u32[]{:S(2)}, u32[]{:S(2)}) collective-permute-start(f32[96,128]{1,0:T(8,128)S(1)} %fusion.3), channel_id=1, source_target_pairs={{0,4},{1,5},{2,6},{3,7},{4,0},{5,1},{6,2},{7,3},{8,12},{9,13},{10,... | collective-permute-start | bytes 147464 | tf_op jit(solution)/shard_map/ppermute | solution.py:268
  15.8 5.2 %collective-permute-start.4 = (f32[168,128]{1,0:T(8,128)S(1)}, f32[168,128]{1,0:T(8,128)S(1)}, u32[]{:S(2)}, u32[]{:S(2)}) collective-permute-start(f32[168,128]{1,0:T(8,128)S(1)} %pad_maximum_fusion), channel_id=1, source_target_pairs={{0,2},{1,3},{2,0},{3,1},{4,6},{5,7},{6,4},{7,5},{8,10},{9,11},{10,... | collective-permute-start | bytes 258056 | tf_op jit(solution)/shard_map/ppermute | solution.py:268
  17.4 6.2 %collective-permute-start.12 = (f32[96,128]{1,0:T(8,128)S(1)}, f32[96,128]{1,0:T(8,128)S(1)}, u32[]{:S(2)}, u32[]{:S(2)}) collective-permute-start(f32[96,128]{1,0:T(8,128)S(1)} %multiply_add_fusion.1), channel_id=1, source_target_pairs={{0,3},{1,2},{2,1},{3,0},{4,7},{5,6},{6,5},{7,4},{8,11},{9,10},{10,... | collective-permute-start | bytes 147464 | tf_op jit(solution)/shard_map/ppermute | solution.py:268
  19.4 4.8 %collective-permute-start.11 = (f32[96,128]{1,0:T(8,128)S(1)}, f32[96,128]{1,0:T(8,128)S(1)}, u32[]{:S(2)}, u32[]{:S(2)}) collective-permute-start(f32[96,128]{1,0:T(8,128)S(1)} %multiply_add_fusion.1), channel_id=1, source_target_pairs={{0,2},{1,3},{2,0},{3,1},{4,6},{5,7},{6,4},{7,5},{8,10},{9,11},{10,... | collective-permute-start | bytes 147464 | tf_op jit(solution)/shard_map/ppermute | solution.py:268
  20.4 4.1 %collective-permute-start.10 = (f32[96,128]{1,0:T(8,128)S(1)}, f32[96,128]{1,0:T(8,128)S(1)}, u32[]{:S(2)}, u32[]{:S(2)}) collective-permute-start(f32[96,128]{1,0:T(8,128)S(1)} %multiply_add_fusion.1), channel_id=1, source_target_pairs={{0,1},{1,0},{2,3},{3,2},{4,5},{5,4},{6,7},{7,6},{8,9},{9,8},{10,11... | collective-permute-start | bytes 147464 | tf_op jit(solution)/shard_map/ppermute | solution.py:268
  21.0 5.5 %collective-permute-start.5 = (f32[168,128]{1,0:T(8,128)S(1)}, f32[168,128]{1,0:T(8,128)S(1)}, u32[]{:S(2)}, u32[]{:S(2)}) collective-permute-start(f32[168,128]{1,0:T(8,128)S(1)} %pad_maximum_fusion.1), channel_id=1, source_target_pairs={{0,4},{1,5},{2,6},{3,7},{4,0},{5,1},{6,2},{7,3},{8,12},{9,13},{10,... | collective-permute-start | bytes 258056 | tf_op jit(solution)/shard_map/ppermute | solution.py:268
where the time goes:
time: 27.3 us; the launch traced here: 27.2 us
  starting transfers between devices  17.7 us (65%)
  Pallas kernels  4.31 us (16%)
  waiting for transfers between devices  4.26 us (16%)
  other arithmetic  0.81 us (3%)
    ppermute x13, starting transfers between devices, exchange(): lax.ppermute(message, ('row', 'col'), [(i, i ^ mask) for i in range(rows...  17.7 us
    pallas_call x1, Pallas kernels, transform_local(): pl.pallas_call(functools.partial(transform_kernel, row_axis), out_shape=p...  4.31 us
    ppermute x13, waiting for transfers between devices, exchange(): lax.ppermute(message, ('row', 'col'), [(i, i ^ mask) for i in range(rows...  4.26 us
    div x1, other arithmetic, local(): return (values * 2.0 ** (measured_qubits / 2) / total).reshape(1, -1)  0.67 us
  transfers between devices with their start and end apart: 13, of which 6 were waited for; matrix products, arithmetic and copies ran while one was open for 0% of the time, Pallas kernels for 0%

commit v1 on v0

--- a/solution.py
+++ b/solution.py
@@ -54,7 +54,7 @@
 
 
 def transform_kernel(
-    row_axis, order_in, amps, messages, buf, out, xs, hlane,
+    row_axis, order_in, amps, messages, buf, out, xs, hlane, row_signs,
     order, inverse, rows_moved, lanes_moved, row_target, row_unit, lane_unit, order_sem, sems,
 ):
     parts, groups, length = buf.shape[0], buf.shape[1] // SUB, buf.shape[2]
@@ -120,7 +120,7 @@
         rank = rank + crosses.astype(jnp.int32)
 
     flips = [bit_of(row_flip, r) == 1 for r in range(row_bits)]
-    out_flips = [bit_of(out_row_flip, r) == 1 for r in range(row_bits)]
+    row_signs[...] = parity_sign(jnp.bitwise_and(iota((ROW_SIDE, LANES), 0), out_row_flip), row_bits)
     sources, gathers = [jnp.int32(0)], [jnp.int32(0)]
     for r in range(row_bits):
         sources = sources + [source + row_unit[r] for source in sources]
@@ -150,11 +150,6 @@
             tiles = merged
         return tiles[0]
 
-    def flip_rows(rows, which):
-        for r in range(row_bits):
-            rows = [jnp.where(which[r], rows[i ^ 1 << r], rows[i]) for i in range(ROW_SIDE)]
-        return rows
-
     def butterfly(blocks, stride):
         return [
             blocks[c ^ stride] - blocks[c] if c & stride else blocks[c] + blocks[c ^ stride] for c in range(len(blocks))
@@ -173,11 +168,13 @@
         return total
 
     def transform(c):
-        rows = flip_rows([xs[source] for source in sources], flips)
+        rows = [xs[source] for source in sources]
+        for r in range(row_bits):
+            rows = [jnp.where(flips[r], rows[i ^ 1 << r], rows[i]) for i in range(ROW_SIDE)]
         rows = [jnp.take_along_axis(rows[i], gathers[i], axis=1) for i in range(ROW_SIDE)]
-        rows = flip_rows(rows, out_flips)
         for r in range(row_bits):
             rows = butterfly(rows, 1 << r)
+        rows = [rows[i] * row_signs[i : i + 1, :] for i in range(ROW_SIDE)]
         rows = [
             jnp.concatenate(butterfly([row[upper * SUB : (upper + 1) * SUB] for upper in range(2)], 1), axis=0)
             for row in rows
@@ -188,8 +185,8 @@
             out[pl.ds(first + i, ROW_SIDE, stride=ROW_SIDE), :] = z[i * ROW_SIDE : (i + 1) * ROW_SIDE]
 
     def one_chunk(c, total):
+        transform(c - 1)
         arrive(2 * c)
-        transform(c - 1)
         total = sums(2 * c, 0, total)
         arrive(2 * c + 1)
         return sums(2 * c + 1, 1, total)
@@ -253,6 +250,7 @@
             pltpu.VMEM((chunks * side, LANES), jnp.float32),
             pltpu.VMEM((ROW_SIDE, ROW_SIDE, LANES), jnp.float32),
             pltpu.VMEM((2 * LANES, LANES), jnp.bfloat16),
+            pltpu.VMEM((ROW_SIDE, LANES), jnp.float32),
             pltpu.SMEM((count,), jnp.int32),
             *[pltpu.SMEM((count + 1,), jnp.int32) for _ in range(6)],
             pltpu.SemaphoreType.DMA(()),

time: 27.3 us -> 27.2 us (level)
  no operation moved by 1% of the time
where the time goes in v1:
time: 27.2 us; the launch traced here: 27 us
  starting transfers between devices  17.7 us (65%)
  waiting for transfers between devices  4.26 us (16%)
  Pallas kernels  4.15 us (15%)
  other arithmetic  0.81 us (3%)
    ppermute x13, starting transfers between devices, exchange(): lax.ppermute(message, ('row', 'col'), [(i, i ^ mask) for i in range(rows...  17.7 us
    ppermute x13, waiting for transfers between devices, exchange(): lax.ppermute(message, ('row', 'col'), [(i, i ^ mask) for i in range(rows...  4.26 us
    pallas_call x1, Pallas kernels, transform_local(): pl.pallas_call(functools.partial(transform_kernel, row_axis), out_shape=p...  4.15 us
    div x1, other arithmetic, local(): return (values * 2.0 ** (measured_qubits / 2) / total).reshape(1, -1)  0.67 us
  transfers between devices with their start and end apart: 13, of which 6 were waited for; matrix products, arithmetic and copies ran while one was open for 0% of the time, Pallas kernels for 0%

profile of v1, /device:TPU:0, one launch (start us, length us, event | category | flops | bytes accessed | tf_op | source)
XLA Modules:
  0.0 27.0 jit_solution(16783350484700360187)
XLA Ops:
  0.0 4.1 %transform_local.1 = f32[1056,128]{1,0:T(8,128)S(1)} custom-call(s32[11]{0:T(128)} %order_in.1, f32[2,8,131072]{2,1,0:T(8,128)} %amps.1), custom_call_target="tpu_custom_call" | custom-call | tf_op jit(solution)/shard_map/transform_local/pallas_call | solution.py:243
  4.2 0.6 %collective-permute-start = (f32[336,128]{1,0:T(8,128)S(1)}, f32[336,128]{1,0:T(8,128)S(1)}, u32[]{:S(2)}, u32[]{:S(2)}) collective-permute-start(f32[336,128]{1,0:T(8,128)S(1)} %concatenate.16), channel_id=1, source_target_pairs={{0,8},{1,9},{2,10},{3,11},{4,12},{5,13},{6,14},{7,15},{8,0},{9,1},... | collective-permute-start | bytes 516104 | tf_op jit(solution)/shard_map/ppermute | solution.py:266
  4.7 0.1 collective-permute-start.6
  4.8 2.7 %collective-permute-start.8 = (f32[96,128]{1,0:T(8,128)S(1)}, f32[96,128]{1,0:T(8,128)S(1)}, u32[]{:S(2)}, u32[]{:S(2)}) collective-permute-start(f32[96,128]{1,0:T(8,128)S(1)} %get-tuple-element.8), channel_id=1, source_target_pairs={{0,24},{1,25},{2,26},{3,27},{4,28},{5,29},{6,30},{7,31},{8,16},{9,... | collective-permute-start | bytes 147464 | tf_op jit(solution)/shard_map/ppermute | solution.py:266
  7.5 0.3 %collective-permute-start.7 = (f32[96,128]{1,0:T(8,128)S(1)}, f32[96,128]{1,0:T(8,128)S(1)}, u32[]{:S(2)}, u32[]{:S(2)}) collective-permute-start(f32[96,128]{1,0:T(8,128)S(1)} %get-tuple-element.9), channel_id=1, source_target_pairs={{0,16},{1,17},{2,18},{3,19},{4,20},{5,21},{6,22},{7,23},{8,24},{9,... | collective-permute-start | bytes 147464 | tf_op jit(solution)/shard_map/ppermute | solution.py:266
  7.8 0.0 collective-permute-done
  7.9 2.7 %collective-permute-start.3 = (f32[168,128]{1,0:T(8,128)S(1)}, f32[168,128]{1,0:T(8,128)S(1)}, u32[]{:S(2)}, u32[]{:S(2)}) collective-permute-start(f32[168,128]{1,0:T(8,128)S(1)} %get-tuple-element.6), channel_id=1, source_target_pairs={{0,17},{1,16},{2,19},{3,18},{4,21},{5,20},{6,23},{7,22},{8,25},{9,... | collective-permute-start | bytes 258056 | tf_op jit(solution)/shard_map/ppermute | solution.py:266
  10.6 0.5 %collective-permute-start.2 = (f32[168,128]{1,0:T(8,128)S(1)}, f32[168,128]{1,0:T(8,128)S(1)}, u32[]{:S(2)}, u32[]{:S(2)}) collective-permute-start(f32[168,128]{1,0:T(8,128)S(1)} %get-tuple-element.6), channel_id=1, source_target_pairs={{0,16},{1,17},{2,18},{3,19},{4,20},{5,21},{6,22},{7,23},{8,24},{9,... | collective-permute-start | bytes 258056 | tf_op jit(solution)/shard_map/ppermute | solution.py:266
  11.1 0.0 collective-permute-done.6
  11.1 0.3 %collective-permute-start.1 = (f32[168,128]{1,0:T(8,128)S(1)}, f32[168,128]{1,0:T(8,128)S(1)}, u32[]{:S(2)}, u32[]{:S(2)}) collective-permute-start(f32[168,128]{1,0:T(8,128)S(1)} %get-tuple-element.5), channel_id=1, source_target_pairs={{0,1},{1,0},{2,3},{3,2},{4,5},{5,4},{6,7},{7,6},{8,9},{9,8},{10,11... | collective-permute-start | bytes 258056 | tf_op jit(solution)/shard_map/ppermute | solution.py:266
  11.4 0.0 collective-permute-done.8
  11.4 0.2 collective-permute-done.7
  11.6 2.7 %collective-permute-start.9 = (f32[96,128]{1,0:T(8,128)S(1)}, f32[96,128]{1,0:T(8,128)S(1)}, u32[]{:S(2)}, u32[]{:S(2)}) collective-permute-start(f32[96,128]{1,0:T(8,128)S(1)} %fusion.3), channel_id=1, source_target_pairs={{0,4},{1,5},{2,6},{3,7},{4,0},{5,1},{6,2},{7,3},{8,12},{9,13},{10,... | collective-permute-start | bytes 147464 | tf_op jit(solution)/shard_map/ppermute | solution.py:266
  14.3 0.0 collective-permute-done.3
  14.3 1.0 %collective-permute-done.2 = f32[168,128]{1,0:T(8,128)S(1)} collective-permute-done((f32[168,128]{1,0:T(8,128)S(1)}, f32[168,128]{1,0:T(8,128)S(1)}, u32[]{:S(2)}, u32[]{:S(2)}) %collective-permute-start.2) | collective-permute-done | bytes 86048 | tf_op jit(solution)/shard_map/ppermute | solution.py:266
  15.3 0.3 collective-permute-done.1
  15.6 1.6 %collective-permute-start.4 = (f32[168,128]{1,0:T(8,128)S(1)}, f32[168,128]{1,0:T(8,128)S(1)}, u32[]{:S(2)}, u32[]{:S(2)}) collective-permute-start(f32[168,128]{1,0:T(8,128)S(1)} %pad_maximum_fusion), channel_id=1, source_target_pairs={{0,2},{1,3},{2,0},{3,1},{4,6},{5,7},{6,4},{7,5},{8,10},{9,11},{10,... | collective-permute-start | bytes 258056 | tf_op jit(solution)/shard_map/ppermute | solution.py:266
  17.2 0.0 collective-permute-done.9
  17.3 2.0 %collective-permute-start.12 = (f32[96,128]{1,0:T(8,128)S(1)}, f32[96,128]{1,0:T(8,128)S(1)}, u32[]{:S(2)}, u32[]{:S(2)}) collective-permute-start(f32[96,128]{1,0:T(8,128)S(1)} %multiply_add_fusion.1), channel_id=1, source_target_pairs={{0,3},{1,2},{2,1},{3,0},{4,7},{5,6},{6,5},{7,4},{8,11},{9,10},{10,... | collective-permute-start | bytes 147464 | tf_op jit(solution)/shard_map/ppermute | solution.py:266
  19.3 1.0 %collective-permute-start.11 = (f32[96,128]{1,0:T(8,128)S(1)}, f32[96,128]{1,0:T(8,128)S(1)}, u32[]{:S(2)}, u32[]{:S(2)}) collective-permute-start(f32[96,128]{1,0:T(8,128)S(1)} %multiply_add_fusion.1), channel_id=1, source_target_pairs={{0,2},{1,3},{2,0},{3,1},{4,6},{5,7},{6,4},{7,5},{8,10},{9,11},{10,... | collective-permute-start | bytes 147464 | tf_op jit(solution)/shard_map/ppermute | solution.py:266
  20.3 0.5 %collective-permute-start.10 = (f32[96,128]{1,0:T(8,128)S(1)}, f32[96,128]{1,0:T(8,128)S(1)}, u32[]{:S(2)}, u32[]{:S(2)}) collective-permute-start(f32[96,128]{1,0:T(8,128)S(1)} %multiply_add_fusion.1), channel_id=1, source_target_pairs={{0,1},{1,0},{2,3},{3,2},{4,5},{5,4},{6,7},{7,6},{8,9},{9,8},{10,11... | collective-permute-start | bytes 147464 | tf_op jit(solution)/shard_map/ppermute | solution.py:266
  20.8 0.0 collective-permute-done.4
  20.9 2.7 %collective-permute-start.5 = (f32[168,128]{1,0:T(8,128)S(1)}, f32[168,128]{1,0:T(8,128)S(1)}, u32[]{:S(2)}, u32[]{:S(2)}) collective-permute-start(f32[168,128]{1,0:T(8,128)S(1)} %pad_maximum_fusion.1), channel_id=1, source_target_pairs={{0,4},{1,5},{2,6},{3,7},{4,0},{5,1},{6,2},{7,3},{8,12},{9,13},{10,... | collective-permute-start | bytes 258056 | tf_op jit(solution)/shard_map/ppermute | solution.py:266
  23.5 0.0 collective-permute-done.12
  23.5 0.5 %collective-permute-done.11 = f32[96,128]{1,0:T(8,128)S(1)} collective-permute-done((f32[96,128]{1,0:T(8,128)S(1)}, f32[96,128]{1,0:T(8,128)S(1)}, u32[]{:S(2)}, u32[]{:S(2)}) %collective-permute-start.11) | collective-permute-done | bytes 49184 | tf_op jit(solution)/shard_map/ppermute | solution.py:266
  24.1 0.3 %collective-permute-done.10 = f32[96,128]{1,0:T(8,128)S(1)} collective-permute-done((f32[96,128]{1,0:T(8,128)S(1)}, f32[96,128]{1,0:T(8,128)S(1)}, u32[]{:S(2)}, u32[]{:S(2)}) %collective-permute-start.10) | collective-permute-done | bytes 49184 | tf_op jit(solution)/shard_map/ppermute | solution.py:266
  24.4 1.9 %collective-permute-done.5 = f32[168,128]{1,0:T(8,128)S(1)} collective-permute-done((f32[168,128]{1,0:T(8,128)S(1)}, f32[168,128]{1,0:T(8,128)S(1)}, u32[]{:S(2)}, u32[]{:S(2)}) %collective-permute-start.5) | collective-permute-done | bytes 86048 | tf_op jit(solution)/shard_map/ppermute | solution.py:266
  26.3 0.7 %fusion = f32[256,128]{1,0:T(8,128)} fusion(f32[96,128]{1,0:T(8,128)S(1)} %fusion.4, f32[160,128]{1,0:T(8,128)S(1)} %slice_add_fusion.2, f32[128]{0:T(128)S(1)} %slice_bitcast_fusion), kind=kLoop, calls=%fused_computation.1 | loop fusion | flops 98304 | bytes 262656 | tf_op jit(solution)/shard_map/div | solution.py:328
  (15 shorter events, 0.2 us)
Async XLA Ops:
  4.2 3.7 %collective-permute-start = (f32[336,128]{1,0:T(8,128)S(1)}, f32[336,128]{1,0:T(8,128)S(1)}, u32[]{:S(2)}, u32[]{:S(2)}) collective-permute-start(f32[336,128]{1,0:T(8,128)S(1)} %concatenate.16), channel_id=1, source_target_pairs={{0,8},{1,9},{2,10},{3,11},{4,12},{5,13},{6,14},{7,15},{8,0},{9,1},... | collective-permute-start | bytes 516104 | tf_op jit(solution)/shard_map/ppermute | solution.py:266
  4.7 6.3 %collective-permute-start.6 = (f32[96,128]{1,0:T(8,128)S(1)}, f32[96,128]{1,0:T(8,128)S(1)}, u32[]{:S(2)}, u32[]{:S(2)}) collective-permute-start(f32[96,128]{1,0:T(8,128)S(1)} %get-tuple-element.7), channel_id=1, source_target_pairs={{0,8},{1,9},{2,10},{3,11},{4,12},{5,13},{6,14},{7,15},{8,0},{9,1},... | collective-permute-start | bytes 147464 | tf_op jit(solution)/shard_map/ppermute | solution.py:266
  4.8 6.6 %collective-permute-start.8 = (f32[96,128]{1,0:T(8,128)S(1)}, f32[96,128]{1,0:T(8,128)S(1)}, u32[]{:S(2)}, u32[]{:S(2)}) collective-permute-start(f32[96,128]{1,0:T(8,128)S(1)} %get-tuple-element.8), channel_id=1, source_target_pairs={{0,24},{1,25},{2,26},{3,27},{4,28},{5,29},{6,30},{7,31},{8,16},{9,... | collective-permute-start | bytes 147464 | tf_op jit(solution)/shard_map/ppermute | solution.py:266
  7.5 4.1 %collective-permute-start.7 = (f32[96,128]{1,0:T(8,128)S(1)}, f32[96,128]{1,0:T(8,128)S(1)}, u32[]{:S(2)}, u32[]{:S(2)}) collective-permute-start(f32[96,128]{1,0:T(8,128)S(1)} %get-tuple-element.9), channel_id=1, source_target_pairs={{0,16},{1,17},{2,18},{3,19},{4,20},{5,21},{6,22},{7,23},{8,24},{9,... | collective-permute-start | bytes 147464 | tf_op jit(solution)/shard_map/ppermute | solution.py:266
  7.9 6.4 %collective-permute-start.3 = (f32[168,128]{1,0:T(8,128)S(1)}, f32[168,128]{1,0:T(8,128)S(1)}, u32[]{:S(2)}, u32[]{:S(2)}) collective-permute-start(f32[168,128]{1,0:T(8,128)S(1)} %get-tuple-element.6), channel_id=1, source_target_pairs={{0,17},{1,16},{2,19},{3,18},{4,21},{5,20},{6,23},{7,22},{8,25},{9,... | collective-permute-start | bytes 258056 | tf_op jit(solution)/shard_map/ppermute | solution.py:266
  10.6 4.7 %collective-permute-start.2 = (f32[168,128]{1,0:T(8,128)S(1)}, f32[168,128]{1,0:T(8,128)S(1)}, u32[]{:S(2)}, u32[]{:S(2)}) collective-permute-start(f32[168,128]{1,0:T(8,128)S(1)} %get-tuple-element.6), channel_id=1, source_target_pairs={{0,16},{1,17},{2,18},{3,19},{4,20},{5,21},{6,22},{7,23},{8,24},{9,... | collective-permute-start | bytes 258056 | tf_op jit(solution)/shard_map/ppermute | solution.py:266
  11.1 4.5 %collective-permute-start.1 = (f32[168,128]{1,0:T(8,128)S(1)}, f32[168,128]{1,0:T(8,128)S(1)}, u32[]{:S(2)}, u32[]{:S(2)}) collective-permute-start(f32[168,128]{1,0:T(8,128)S(1)} %get-tuple-element.5), channel_id=1, source_target_pairs={{0,1},{1,0},{2,3},{3,2},{4,5},{5,4},{6,7},{7,6},{8,9},{9,8},{10,11... | collective-permute-start | bytes 258056 | tf_op jit(solution)/shard_map/ppermute | solution.py:266
  11.6 5.6 %collective-permute-start.9 = (f32[96,128]{1,0:T(8,128)S(1)}, f32[96,128]{1,0:T(8,128)S(1)}, u32[]{:S(2)}, u32[]{:S(2)}) collective-permute-start(f32[96,128]{1,0:T(8,128)S(1)} %fusion.3), channel_id=1, source_target_pairs={{0,4},{1,5},{2,6},{3,7},{4,0},{5,1},{6,2},{7,3},{8,12},{9,13},{10,... | collective-permute-start | bytes 147464 | tf_op jit(solution)/shard_map/ppermute | solution.py:266
  15.6 5.2 %collective-permute-start.4 = (f32[168,128]{1,0:T(8,128)S(1)}, f32[168,128]{1,0:T(8,128)S(1)}, u32[]{:S(2)}, u32[]{:S(2)}) collective-permute-start(f32[168,128]{1,0:T(8,128)S(1)} %pad_maximum_fusion), channel_id=1, source_target_pairs={{0,2},{1,3},{2,0},{3,1},{4,6},{5,7},{6,4},{7,5},{8,10},{9,11},{10,... | collective-permute-start | bytes 258056 | tf_op jit(solution)/shard_map/ppermute | solution.py:266
  17.3 6.3 %collective-permute-start.12 = (f32[96,128]{1,0:T(8,128)S(1)}, f32[96,128]{1,0:T(8,128)S(1)}, u32[]{:S(2)}, u32[]{:S(2)}) collective-permute-start(f32[96,128]{1,0:T(8,128)S(1)} %multiply_add_fusion.1), channel_id=1, source_target_pairs={{0,3},{1,2},{2,1},{3,0},{4,7},{5,6},{6,5},{7,4},{8,11},{9,10},{10,... | collective-permute-start | bytes 147464 | tf_op jit(solution)/shard_map/ppermute | solution.py:266
  19.3 4.8 %collective-permute-start.11 = (f32[96,128]{1,0:T(8,128)S(1)}, f32[96,128]{1,0:T(8,128)S(1)}, u32[]{:S(2)}, u32[]{:S(2)}) collective-permute-start(f32[96,128]{1,0:T(8,128)S(1)} %multiply_add_fusion.1), channel_id=1, source_target_pairs={{0,2},{1,3},{2,0},{3,1},{4,6},{5,7},{6,4},{7,5},{8,10},{9,11},{10,... | collective-permute-start | bytes 147464 | tf_op jit(solution)/shard_map/ppermute | solution.py:266
  20.3 4.1 %collective-permute-start.10 = (f32[96,128]{1,0:T(8,128)S(1)}, f32[96,128]{1,0:T(8,128)S(1)}, u32[]{:S(2)}, u32[]{:S(2)}) collective-permute-start(f32[96,128]{1,0:T(8,128)S(1)} %multiply_add_fusion.1), channel_id=1, source_target_pairs={{0,1},{1,0},{2,3},{3,2},{4,5},{5,4},{6,7},{7,6},{8,9},{9,8},{10,11... | collective-permute-start | bytes 147464 | tf_op jit(solution)/shard_map/ppermute | solution.py:266
  20.9 5.5 %collective-permute-start.5 = (f32[168,128]{1,0:T(8,128)S(1)}, f32[168,128]{1,0:T(8,128)S(1)}, u32[]{:S(2)}, u32[]{:S(2)}) collective-permute-start(f32[168,128]{1,0:T(8,128)S(1)} %pad_maximum_fusion.1), channel_id=1, source_target_pairs={{0,4},{1,5},{2,6},{3,7},{4,0},{5,1},{6,2},{7,3},{8,12},{9,13},{10,... | collective-permute-start | bytes 258056 | tf_op jit(solution)/shard_map/ppermute | solution.py:266

commit v2 on v1

--- a/solution.py
+++ b/solution.py
@@ -9,7 +9,7 @@
 
 
 LANES = 128
-FIRST_PART = 5
+FIRST_PART = 10
 SUB = 8
 ROW_SIDE = 16
 CHUNK = ROW_SIDE * ROW_SIDE * LANES
@@ -28,8 +28,8 @@
 
 
 def first_rows(share):
-    unit = 4 * SUB if share % (8 * SUB) == 0 else SUB
-    return share * FIRST_PART // 8 // unit * unit
+    unit = 2 * SUB if share % (4 * SUB) == 0 else SUB
+    return share * FIRST_PART // 16 // unit * unit
 
 
 def block_order(count):
@@ -212,7 +212,7 @@
         return blocks * (first + SUB) + at * (share - first) + row - first
 
     signs = [parity_sign(jnp.bitwise_and(own, c), log2(blocks)) for c in range(chunks)]
-    rows = 4 * SUB
+    rows = 2 * SUB
     for start in range(0, side, rows):
         levels = [out[c * side + start : c * side + start + rows, :] for c in range(chunks)]
         if blocks == chunks:

time: 27.2 us -> 27.2 us (level)
  no operation moved by 1% of the time
where the time goes in v2:
time: 27.2 us; the launch traced here: 27 us
  starting transfers between devices  17.7 us (65%)
  waiting for transfers between devices  4.26 us (16%)
  Pallas kernels  4.15 us (15%)
  other arithmetic  0.81 us (3%)
    ppermute x13, starting transfers between devices, exchange(): lax.ppermute(message, ('row', 'col'), [(i, i ^ mask) for i in range(rows...  17.7 us
    ppermute x13, waiting for transfers between devices, exchange(): lax.ppermute(message, ('row', 'col'), [(i, i ^ mask) for i in range(rows...  4.26 us
    pallas_call x1, Pallas kernels, transform_local(): pl.pallas_call(functools.partial(transform_kernel, row_axis), out_shape=p...  4.15 us
    div x1, other arithmetic, local(): return (values * 2.0 ** (measured_qubits / 2) / total).reshape(1, -1)  0.67 us
  transfers between devices with their start and end apart: 13, of which 6 were waited for; matrix products, arithmetic and copies ran while one was open for 0% of the time, Pallas kernels for 0%

profile of v2, /device:TPU:0, one launch (start us, length us, event | category | flops | bytes accessed | tf_op | source)
XLA Modules:
  0.0 27.0 jit_solution(9554475415930067205)
XLA Ops:
  0.0 4.1 %transform_local.1 = f32[1056,128]{1,0:T(8,128)S(1)} custom-call(s32[11]{0:T(128)} %order_in.1, f32[2,8,131072]{2,1,0:T(8,128)} %amps.1), custom_call_target="tpu_custom_call" | custom-call | tf_op jit(solution)/shard_map/transform_local/pallas_call | solution.py:243
  4.2 0.6 %collective-permute-start = (f32[336,128]{1,0:T(8,128)S(1)}, f32[336,128]{1,0:T(8,128)S(1)}, u32[]{:S(2)}, u32[]{:S(2)}) collective-permute-start(f32[336,128]{1,0:T(8,128)S(1)} %concatenate.16), channel_id=1, source_target_pairs={{0,8},{1,9},{2,10},{3,11},{4,12},{5,13},{6,14},{7,15},{8,0},{9,1},... | collective-permute-start | bytes 516104 | tf_op jit(solution)/shard_map/ppermute | solution.py:266
  4.7 0.1 collective-permute-start.6
  4.8 2.7 %collective-permute-start.8 = (f32[96,128]{1,0:T(8,128)S(1)}, f32[96,128]{1,0:T(8,128)S(1)}, u32[]{:S(2)}, u32[]{:S(2)}) collective-permute-start(f32[96,128]{1,0:T(8,128)S(1)} %get-tuple-element.8), channel_id=1, source_target_pairs={{0,24},{1,25},{2,26},{3,27},{4,28},{5,29},{6,30},{7,31},{8,16},{9,... | collective-permute-start | bytes 147464 | tf_op jit(solution)/shard_map/ppermute | solution.py:266
  7.5 0.3 %collective-permute-start.7 = (f32[96,128]{1,0:T(8,128)S(1)}, f32[96,128]{1,0:T(8,128)S(1)}, u32[]{:S(2)}, u32[]{:S(2)}) collective-permute-start(f32[96,128]{1,0:T(8,128)S(1)} %get-tuple-element.9), channel_id=1, source_target_pairs={{0,16},{1,17},{2,18},{3,19},{4,20},{5,21},{6,22},{7,23},{8,24},{9,... | collective-permute-start | bytes 147464 | tf_op jit(solution)/shard_map/ppermute | solution.py:266
  7.8 0.0 collective-permute-done
  7.9 2.7 %collective-permute-start.3 = (f32[168,128]{1,0:T(8,128)S(1)}, f32[168,128]{1,0:T(8,128)S(1)}, u32[]{:S(2)}, u32[]{:S(2)}) collective-permute-start(f32[168,128]{1,0:T(8,128)S(1)} %get-tuple-element.6), channel_id=1, source_target_pairs={{0,17},{1,16},{2,19},{3,18},{4,21},{5,20},{6,23},{7,22},{8,25},{9,... | collective-permute-start | bytes 258056 | tf_op jit(solution)/shard_map/ppermute | solution.py:266
  10.6 0.5 %collective-permute-start.2 = (f32[168,128]{1,0:T(8,128)S(1)}, f32[168,128]{1,0:T(8,128)S(1)}, u32[]{:S(2)}, u32[]{:S(2)}) collective-permute-start(f32[168,128]{1,0:T(8,128)S(1)} %get-tuple-element.6), channel_id=1, source_target_pairs={{0,16},{1,17},{2,18},{3,19},{4,20},{5,21},{6,22},{7,23},{8,24},{9,... | collective-permute-start | bytes 258056 | tf_op jit(solution)/shard_map/ppermute | solution.py:266
  11.1 0.0 collective-permute-done.6
  11.1 0.3 %collective-permute-start.1 = (f32[168,128]{1,0:T(8,128)S(1)}, f32[168,128]{1,0:T(8,128)S(1)}, u32[]{:S(2)}, u32[]{:S(2)}) collective-permute-start(f32[168,128]{1,0:T(8,128)S(1)} %get-tuple-element.5), channel_id=1, source_target_pairs={{0,1},{1,0},{2,3},{3,2},{4,5},{5,4},{6,7},{7,6},{8,9},{9,8},{10,11... | collective-permute-start | bytes 258056 | tf_op jit(solution)/shard_map/ppermute | solution.py:266
  11.4 0.0 collective-permute-done.8
  11.4 0.2 collective-permute-done.7
  11.6 2.7 %collective-permute-start.9 = (f32[96,128]{1,0:T(8,128)S(1)}, f32[96,128]{1,0:T(8,128)S(1)}, u32[]{:S(2)}, u32[]{:S(2)}) collective-permute-start(f32[96,128]{1,0:T(8,128)S(1)} %fusion.3), channel_id=1, source_target_pairs={{0,4},{1,5},{2,6},{3,7},{4,0},{5,1},{6,2},{7,3},{8,12},{9,13},{10,... | collective-permute-start | bytes 147464 | tf_op jit(solution)/shard_map/ppermute | solution.py:266
  14.3 0.0 collective-permute-done.3
  14.3 1.0 %collective-permute-done.2 = f32[168,128]{1,0:T(8,128)S(1)} collective-permute-done((f32[168,128]{1,0:T(8,128)S(1)}, f32[168,128]{1,0:T(8,128)S(1)}, u32[]{:S(2)}, u32[]{:S(2)}) %collective-permute-start.2) | collective-permute-done | bytes 86048 | tf_op jit(solution)/shard_map/ppermute | solution.py:266
  15.3 0.3 collective-permute-done.1
  15.6 1.6 %collective-permute-start.4 = (f32[168,128]{1,0:T(8,128)S(1)}, f32[168,128]{1,0:T(8,128)S(1)}, u32[]{:S(2)}, u32[]{:S(2)}) collective-permute-start(f32[168,128]{1,0:T(8,128)S(1)} %pad_maximum_fusion), channel_id=1, source_target_pairs={{0,2},{1,3},{2,0},{3,1},{4,6},{5,7},{6,4},{7,5},{8,10},{9,11},{10,... | collective-permute-start | bytes 258056 | tf_op jit(solution)/shard_map/ppermute | solution.py:266
  17.2 0.0 collective-permute-done.9
  17.3 2.0 %collective-permute-start.12 = (f32[96,128]{1,0:T(8,128)S(1)}, f32[96,128]{1,0:T(8,128)S(1)}, u32[]{:S(2)}, u32[]{:S(2)}) collective-permute-start(f32[96,128]{1,0:T(8,128)S(1)} %multiply_add_fusion.1), channel_id=1, source_target_pairs={{0,3},{1,2},{2,1},{3,0},{4,7},{5,6},{6,5},{7,4},{8,11},{9,10},{10,... | collective-permute-start | bytes 147464 | tf_op jit(solution)/shard_map/ppermute | solution.py:266
  19.3 1.0 %collective-permute-start.11 = (f32[96,128]{1,0:T(8,128)S(1)}, f32[96,128]{1,0:T(8,128)S(1)}, u32[]{:S(2)}, u32[]{:S(2)}) collective-permute-start(f32[96,128]{1,0:T(8,128)S(1)} %multiply_add_fusion.1), channel_id=1, source_target_pairs={{0,2},{1,3},{2,0},{3,1},{4,6},{5,7},{6,4},{7,5},{8,10},{9,11},{10,... | collective-permute-start | bytes 147464 | tf_op jit(solution)/shard_map/ppermute | solution.py:266
  20.3 0.5 %collective-permute-start.10 = (f32[96,128]{1,0:T(8,128)S(1)}, f32[96,128]{1,0:T(8,128)S(1)}, u32[]{:S(2)}, u32[]{:S(2)}) collective-permute-start(f32[96,128]{1,0:T(8,128)S(1)} %multiply_add_fusion.1), channel_id=1, source_target_pairs={{0,1},{1,0},{2,3},{3,2},{4,5},{5,4},{6,7},{7,6},{8,9},{9,8},{10,11... | collective-permute-start | bytes 147464 | tf_op jit(solution)/shard_map/ppermute | solution.py:266
  20.8 0.0 collective-permute-done.4
  20.9 2.7 %collective-permute-start.5 = (f32[168,128]{1,0:T(8,128)S(1)}, f32[168,128]{1,0:T(8,128)S(1)}, u32[]{:S(2)}, u32[]{:S(2)}) collective-permute-start(f32[168,128]{1,0:T(8,128)S(1)} %pad_maximum_fusion.1), channel_id=1, source_target_pairs={{0,4},{1,5},{2,6},{3,7},{4,0},{5,1},{6,2},{7,3},{8,12},{9,13},{10,... | collective-permute-start | bytes 258056 | tf_op jit(solution)/shard_map/ppermute | solution.py:266
  23.5 0.0 collective-permute-done.12
  23.5 0.5 %collective-permute-done.11 = f32[96,128]{1,0:T(8,128)S(1)} collective-permute-done((f32[96,128]{1,0:T(8,128)S(1)}, f32[96,128]{1,0:T(8,128)S(1)}, u32[]{:S(2)}, u32[]{:S(2)}) %collective-permute-start.11) | collective-permute-done | bytes 49184 | tf_op jit(solution)/shard_map/ppermute | solution.py:266
  24.1 0.3 %collective-permute-done.10 = f32[96,128]{1,0:T(8,128)S(1)} collective-permute-done((f32[96,128]{1,0:T(8,128)S(1)}, f32[96,128]{1,0:T(8,128)S(1)}, u32[]{:S(2)}, u32[]{:S(2)}) %collective-permute-start.10) | collective-permute-done | bytes 49184 | tf_op jit(solution)/shard_map/ppermute | solution.py:266
  24.4 1.9 %collective-permute-done.5 = f32[168,128]{1,0:T(8,128)S(1)} collective-permute-done((f32[168,128]{1,0:T(8,128)S(1)}, f32[168,128]{1,0:T(8,128)S(1)}, u32[]{:S(2)}, u32[]{:S(2)}) %collective-permute-start.5) | collective-permute-done | bytes 86048 | tf_op jit(solution)/shard_map/ppermute | solution.py:266
  26.3 0.7 %fusion = f32[256,128]{1,0:T(8,128)} fusion(f32[96,128]{1,0:T(8,128)S(1)} %fusion.4, f32[160,128]{1,0:T(8,128)S(1)} %slice_add_fusion.2, f32[128]{0:T(128)S(1)} %slice_bitcast_fusion), kind=kLoop, calls=%fused_computation.1 | loop fusion | flops 98304 | bytes 262656 | tf_op jit(solution)/shard_map/div | solution.py:328
  (15 shorter events, 0.2 us)
Async XLA Ops:
  4.2 3.7 %collective-permute-start = (f32[336,128]{1,0:T(8,128)S(1)}, f32[336,128]{1,0:T(8,128)S(1)}, u32[]{:S(2)}, u32[]{:S(2)}) collective-permute-start(f32[336,128]{1,0:T(8,128)S(1)} %concatenate.16), channel_id=1, source_target_pairs={{0,8},{1,9},{2,10},{3,11},{4,12},{5,13},{6,14},{7,15},{8,0},{9,1},... | collective-permute-start | bytes 516104 | tf_op jit(solution)/shard_map/ppermute | solution.py:266
  4.7 6.3 %collective-permute-start.6 = (f32[96,128]{1,0:T(8,128)S(1)}, f32[96,128]{1,0:T(8,128)S(1)}, u32[]{:S(2)}, u32[]{:S(2)}) collective-permute-start(f32[96,128]{1,0:T(8,128)S(1)} %get-tuple-element.7), channel_id=1, source_target_pairs={{0,8},{1,9},{2,10},{3,11},{4,12},{5,13},{6,14},{7,15},{8,0},{9,1},... | collective-permute-start | bytes 147464 | tf_op jit(solution)/shard_map/ppermute | solution.py:266
  4.8 6.6 %collective-permute-start.8 = (f32[96,128]{1,0:T(8,128)S(1)}, f32[96,128]{1,0:T(8,128)S(1)}, u32[]{:S(2)}, u32[]{:S(2)}) collective-permute-start(f32[96,128]{1,0:T(8,128)S(1)} %get-tuple-element.8), channel_id=1, source_target_pairs={{0,24},{1,25},{2,26},{3,27},{4,28},{5,29},{6,30},{7,31},{8,16},{9,... | collective-permute-start | bytes 147464 | tf_op jit(solution)/shard_map/ppermute | solution.py:266
  7.5 4.1 %collective-permute-start.7 = (f32[96,128]{1,0:T(8,128)S(1)}, f32[96,128]{1,0:T(8,128)S(1)}, u32[]{:S(2)}, u32[]{:S(2)}) collective-permute-start(f32[96,128]{1,0:T(8,128)S(1)} %get-tuple-element.9), channel_id=1, source_target_pairs={{0,16},{1,17},{2,18},{3,19},{4,20},{5,21},{6,22},{7,23},{8,24},{9,... | collective-permute-start | bytes 147464 | tf_op jit(solution)/shard_map/ppermute | solution.py:266
  7.9 6.4 %collective-permute-start.3 = (f32[168,128]{1,0:T(8,128)S(1)}, f32[168,128]{1,0:T(8,128)S(1)}, u32[]{:S(2)}, u32[]{:S(2)}) collective-permute-start(f32[168,128]{1,0:T(8,128)S(1)} %get-tuple-element.6), channel_id=1, source_target_pairs={{0,17},{1,16},{2,19},{3,18},{4,21},{5,20},{6,23},{7,22},{8,25},{9,... | collective-permute-start | bytes 258056 | tf_op jit(solution)/shard_map/ppermute | solution.py:266
  10.6 4.7 %collective-permute-start.2 = (f32[168,128]{1,0:T(8,128)S(1)}, f32[168,128]{1,0:T(8,128)S(1)}, u32[]{:S(2)}, u32[]{:S(2)}) collective-permute-start(f32[168,128]{1,0:T(8,128)S(1)} %get-tuple-element.6), channel_id=1, source_target_pairs={{0,16},{1,17},{2,18},{3,19},{4,20},{5,21},{6,22},{7,23},{8,24},{9,... | collective-permute-start | bytes 258056 | tf_op jit(solution)/shard_map/ppermute | solution.py:266
  11.1 4.5 %collective-permute-start.1 = (f32[168,128]{1,0:T(8,128)S(1)}, f32[168,128]{1,0:T(8,128)S(1)}, u32[]{:S(2)}, u32[]{:S(2)}) collective-permute-start(f32[168,128]{1,0:T(8,128)S(1)} %get-tuple-element.5), channel_id=1, source_target_pairs={{0,1},{1,0},{2,3},{3,2},{4,5},{5,4},{6,7},{7,6},{8,9},{9,8},{10,11... | collective-permute-start | bytes 258056 | tf_op jit(solution)/shard_map/ppermute | solution.py:266
  11.6 5.6 %collective-permute-start.9 = (f32[96,128]{1,0:T(8,128)S(1)}, f32[96,128]{1,0:T(8,128)S(1)}, u32[]{:S(2)}, u32[]{:S(2)}) collective-permute-start(f32[96,128]{1,0:T(8,128)S(1)} %fusion.3), channel_id=1, source_target_pairs={{0,4},{1,5},{2,6},{3,7},{4,0},{5,1},{6,2},{7,3},{8,12},{9,13},{10,... | collective-permute-start | bytes 147464 | tf_op jit(solution)/shard_map/ppermute | solution.py:266
  15.6 5.2 %collective-permute-start.4 = (f32[168,128]{1,0:T(8,128)S(1)}, f32[168,128]{1,0:T(8,128)S(1)}, u32[]{:S(2)}, u32[]{:S(2)}) collective-permute-start(f32[168,128]{1,0:T(8,128)S(1)} %pad_maximum_fusion), channel_id=1, source_target_pairs={{0,2},{1,3},{2,0},{3,1},{4,6},{5,7},{6,4},{7,5},{8,10},{9,11},{10,... | collective-permute-start | bytes 258056 | tf_op jit(solution)/shard_map/ppermute | solution.py:266
  17.3 6.3 %collective-permute-start.12 = (f32[96,128]{1,0:T(8,128)S(1)}, f32[96,128]{1,0:T(8,128)S(1)}, u32[]{:S(2)}, u32[]{:S(2)}) collective-permute-start(f32[96,128]{1,0:T(8,128)S(1)} %multiply_add_fusion.1), channel_id=1, source_target_pairs={{0,3},{1,2},{2,1},{3,0},{4,7},{5,6},{6,5},{7,4},{8,11},{9,10},{10,... | collective-permute-start | bytes 147464 | tf_op jit(solution)/shard_map/ppermute | solution.py:266
  19.3 4.8 %collective-permute-start.11 = (f32[96,128]{1,0:T(8,128)S(1)}, f32[96,128]{1,0:T(8,128)S(1)}, u32[]{:S(2)}, u32[]{:S(2)}) collective-permute-start(f32[96,128]{1,0:T(8,128)S(1)} %multiply_add_fusion.1), channel_id=1, source_target_pairs={{0,2},{1,3},{2,0},{3,1},{4,6},{5,7},{6,4},{7,5},{8,10},{9,11},{10,... | collective-permute-start | bytes 147464 | tf_op jit(solution)/shard_map/ppermute | solution.py:266
  20.3 4.1 %collective-permute-start.10 = (f32[96,128]{1,0:T(8,128)S(1)}, f32[96,128]{1,0:T(8,128)S(1)}, u32[]{:S(2)}, u32[]{:S(2)}) collective-permute-start(f32[96,128]{1,0:T(8,128)S(1)} %multiply_add_fusion.1), channel_id=1, source_target_pairs={{0,1},{1,0},{2,3},{3,2},{4,5},{5,4},{6,7},{7,6},{8,9},{9,8},{10,11... | collective-permute-start | bytes 147464 | tf_op jit(solution)/shard_map/ppermute | solution.py:266
  20.9 5.5 %collective-permute-start.5 = (f32[168,128]{1,0:T(8,128)S(1)}, f32[168,128]{1,0:T(8,128)S(1)}, u32[]{:S(2)}, u32[]{:S(2)}) collective-permute-start(f32[168,128]{1,0:T(8,128)S(1)} %pad_maximum_fusion.1), channel_id=1, source_target_pairs={{0,4},{1,5},{2,6},{3,7},{4,0},{5,1},{6,2},{7,3},{8,12},{9,13},{10,... | collective-permute-start | bytes 258056 | tf_op jit(solution)/shard_map/ppermute | solution.py:266
